TPU v7x, 32 devices: a whole 2x2x4 slice. The times are simulated.
32 devices in a mesh: section: 2 (over y), dp: 16 (over z, x, core).
Axes of the slice: x: 2, y: 2, z: 4, core: 2. Of those that a mesh axis runs over, the one named last changes fastest.
Arguments:
- residuals: float32 [8, 128, 4096], P('section', 'dp'), may hold values from -100 to 100, as said below
- owners: int32 [32], replicated, may hold values from 0 to 31, each once
Outputs:
- harvest: bfloat16 [128, 8, 4096], P(('section', 'dp'))
Inputs may be any that keep to these rules, and one draw needn't show every extreme that they name: `owners`: a permutation of the block numbers. `residuals`: real-valued activations.
All inputs are finite; a program needn't handle non-finite values.
Results may differ from a plain program's by a relative error of at most 0.0004.
Values may be sent and summed in bfloat16 or wider, within the bound.
A program may use at most 64 MiB of HBM per device.

v0:
```python
import functools

import jax
import jax.numpy as jnp
from jax import lax
from jax.experimental import pallas as pl
from jax.experimental.pallas import tpu as pltpu
from jax.sharding import PartitionSpec as P

MESH = pl.DeviceIdType.MESH
LANES = 128
SUBLANES = 8


def harvest_kernel(sections, groups, early, x_hbm, owners_hbm, out_ref, owners, inverse, xv, centered, part, parts,
                   late, s1, s2, r2, x_sem, o_sem, e_send, e_recv, send1, recv1, send2, recv2, *r1):
    half = s1.shape[2] // 2
    layers, tokens, features = x_hbm.shape
    chunks, blocks, rows, _ = s1.shape
    width = features // groups
    block_len = rows // layers
    per_dev = tokens // block_len
    devices = sections * groups
    section, group = lax.axis_index("section"), lax.axis_index("dp")
    me = section * groups + group

    load = pltpu.make_async_copy(x_hbm, xv, x_sem)
    load.start()
    barrier = pltpu.get_barrier_semaphore()

    def peer_of(k):
        return lax.rem(group + k, groups)

    for k in range(1, groups):
        pl.semaphore_signal(barrier, inc=1, device_id=(section, peer_of(k)), device_id_type=MESH)
    for k in range(1, sections):
        pl.semaphore_signal(barrier, inc=1, device_id=(lax.rem(section + k, sections), group), device_id_type=MESH)

    load_owners = pltpu.make_async_copy(owners_hbm, owners, o_sem)
    load_owners.start()
    load.wait()
    per_tile = SUBLANES // layers
    lane = lax.broadcasted_iota(jnp.int32, (SUBLANES, LANES), 1)
    row = lax.broadcasted_iota(jnp.int32, (SUBLANES, LANES), 0)
    total = jnp.zeros((SUBLANES, LANES), jnp.float32)
    for l in range(layers):
        acc = jnp.zeros((SUBLANES, LANES), jnp.float32)
        for t in range(0, tokens, SUBLANES):
            x = xv[l, t:t + SUBLANES]
            c = x - jnp.sum(x, axis=1, keepdims=True) * (1.0 / features)
            xv[l, t:t + SUBLANES] = c
            sq = c * c
            for f in range(features // LANES):
                acc = acc + sq[:, f * LANES:(f + 1) * LANES]
        fold = LANES // 2
        while fold >= LANES // layers:
            acc = acc + pltpu.roll(acc, fold, 1)
            fold //= 2
        total = total + jnp.where(lane // (LANES // layers) == l, acc, 0.0)
    own_lanes = lane // (LANES // layers) == row % layers
    acc = jnp.sum(total, axis=0, keepdims=True)
    part[...] = acc
    parts[group] = acc

    pl.semaphore_wait(barrier, groups + sections - 2)
    order = sorted(range(1, groups), key=lambda p: min(p, groups - p))
    early_order = sorted(range(1, groups), key=lambda p: min(p, groups - p))
    first_order = sorted(range(1, groups), key=lambda p: min(p, groups - p))
    second_order = list(range(1, groups))
    for k in order:
        pltpu.make_async_remote_copy(
            src_ref=part, dst_ref=parts.at[group], send_sem=e_send, recv_sem=e_recv,
            device_id=(section, peer_of(k)), device_id_type=MESH).start()

    mine = pl.ds(group * per_dev, per_dev)
    units = len(r1)

    def spread(u, source):
        for p in (early_order if u == chunks else first_order):
            d = peer_of(p)
            pltpu.make_async_remote_copy(
                src_ref=source(d), dst_ref=r1[u].at[mine], send_sem=send1.at[u], recv_sem=recv1.at[u],
                device_id=(section, d), device_id_type=MESH).start()
        r1[u][mine] = source(group)[...]

    def regroup(g):
        j, r = divmod(g * SUBLANES, rows)
        c = jnp.concatenate([xv[:, g * per_tile + i, :] for i in range(per_tile)], axis=0)
        for f in range(features // LANES):
            centered[f, j, r:r + SUBLANES] = c[:, f * LANES:(f + 1) * LANES]

    tiles = range(tokens // per_tile)
    first = [g for g in tiles if g * SUBLANES % rows < half]
    for g in first:
        regroup(g)
    if early:
        spread(chunks, lambda d: centered.at[d * chunks, :, pl.ds(0, half)])

    for g in tiles:
        if g not in first:
            regroup(g)
    load_owners.wait()

    @pl.loop(0, blocks)
    def _(o):
        found = jnp.int32(0)
        for b in range(blocks):
            found = jnp.where(owners[b] == o, jnp.int32(b), found)
        inverse[o] = found

    others = pl.ds(0, groups - 1)
    energy_wait = pltpu.make_async_remote_copy(
        src_ref=parts.at[others], dst_ref=parts.at[others], send_sem=e_send, recv_sem=e_recv,
        device_id=(section, peer_of(1)), device_id_type=MESH)
    energy_wait.wait_recv()
    total = parts[0]
    for g in range(1, groups):
        total = total + parts[g]
    energy = jnp.sum(jnp.where(own_lanes, total, 0.0), axis=1, keepdims=True)
    scale = 1.0 / jnp.sqrt(energy * (1.0 / (tokens * groups * features)) + 1.0)
    scale = jnp.concatenate([scale] * (rows // SUBLANES), axis=0)

    for k in range(chunks):
        top = half if early and k == 0 else 0
        for d in range(groups):
            for j in range(per_dev):
                b = d * per_dev + j
                if top:
                    late[b] = (centered[d * chunks, j, top:] * scale[top:]).astype(jnp.bfloat16)
                else:
                    s1[k, b] = (centered[d * chunks + k, j] * scale).astype(jnp.bfloat16)
        if top:
            spread(k, lambda d: late.at[pl.ds(d * per_dev, per_dev)])
        else:
            spread(k, lambda d: s1.at[k, pl.ds(d * per_dev, per_dev)])

    def arrived(u):
        span = pl.ds(0, (groups - 1) * per_dev)
        return pltpu.make_async_remote_copy(
            src_ref=r1[u].at[span], dst_ref=r1[u].at[span], send_sem=send1.at[u], recv_sem=recv1.at[u],
            device_id=(section, peer_of(1)), device_id_type=MESH)

    routes = [(p, q) for p in second_order + [0] for q in range(sections)]
    lag = 8

    def deliver(u, view):
        def place(p, q):
            sec, d = lax.rem(section + q, sections), peer_of(p)
            return sec, d, sec * groups + d

        def select(p, q):
            o = place(p, q)[2]
            block = r1[u][inverse[o]]
            if u == chunks:
                block = (block * scale[:half]).astype(jnp.bfloat16)
            view(s2 if p or q else r2, o)[...] = block

        def send(p, q):
            if p or q:
                sec, d, o = place(p, q)
                pltpu.make_async_remote_copy(
                    src_ref=view(s2, o), dst_ref=view(r2, me), send_sem=send2.at[u], recv_sem=recv2.at[u],
                    device_id=(sec, d), device_id_type=MESH).start()

        for n in range(len(routes) + lag):
            if n < len(routes):
                select(*routes[n])
            if n >= lag:
                send(*routes[n - lag])

    def view_of(u):
        if u == chunks:
            return lambda ref, at: ref.at[0, at, pl.ds(0, half)]
        if early and u == 0:
            return lambda ref, at: ref.at[0, at, pl.ds(half, half)]
        return lambda ref, at: ref.at[u, at]

    def delivered(u):
        ref = view_of(u)(r2, pl.ds(0, devices - 1))
        return pltpu.make_async_remote_copy(
            src_ref=ref, dst_ref=ref, send_sem=send2.at[u], recv_sem=recv2.at[u],
            device_id=(section, peer_of(1)), device_id_type=MESH)

    for u in ([chunks] if early else []) + list(range(chunks)):
        arrived(u).wait_recv()
        deliver(u, view_of(u))

    for k in range(chunks):
        delivered(k).wait_recv()
        if early and k == 0:
            delivered(chunks).wait_recv()
        for d in range(groups):
            got = [r2[k, s * groups + d].astype(jnp.float32) for s in range(sections)]
            lane = d * width + k * LANES
            for i in range(block_len):
                out_ref[i, :, lane:lane + LANES] = jnp.concatenate(
                    [v[i * layers:(i + 1) * layers] for v in got], axis=0).astype(jnp.bfloat16)
    energy_wait.wait_send()
    for u in range(units):
        arrived(u).wait_send()
        delivered(u).wait_send()


def store_kernel(assembled, out_hbm, sem):
    store = pltpu.make_async_copy(assembled, out_hbm, sem)
    store.start()
    store.wait()


def solution(mesh):
    sections, groups = mesh.shape["section"], mesh.shape["dp"]

    def on_device(residuals, owners):
        layers, tokens, features = residuals.shape
        blocks = owners.shape[0]
        block_len = tokens * groups // blocks
        rows = block_len * layers
        chunks = features // groups // LANES
        early = chunks > 1
        tiles = (chunks, blocks, rows, LANES)
        part_tiles = (blocks, rows // 2, LANES)
        dma = pltpu.SemaphoreType.DMA
        received = pl.pallas_call(
            functools.partial(harvest_kernel, sections, groups, early),
            out_shape=pltpu.VMEM((block_len, layers * sections, features), jnp.bfloat16),
            in_specs=[pl.BlockSpec(memory_space=pl.ANY), pl.BlockSpec(memory_space=pl.ANY)],
            out_specs=pl.BlockSpec(memory_space=pltpu.VMEM),
            scratch_shapes=[
                pltpu.SMEM((blocks,), jnp.int32),
                pltpu.SMEM((blocks,), jnp.int32),
                pltpu.VMEM((layers, tokens, features), jnp.float32),
                pltpu.VMEM((features // LANES, blocks // groups, rows, LANES), jnp.float32),
                pltpu.VMEM((1, LANES), jnp.float32),
                pltpu.VMEM((groups, 1, LANES), jnp.float32),
                pltpu.VMEM(part_tiles, jnp.bfloat16),
                pltpu.VMEM(tiles, jnp.bfloat16),
                pltpu.VMEM(tiles, jnp.bfloat16),
                pltpu.VMEM(tiles, jnp.bfloat16),
                dma, dma, dma, dma,
                *[dma((chunks + early,)) for _ in range(4)],
                *([pltpu.VMEM(part_tiles, jnp.bfloat16)] if early else []),
                *[pltpu.VMEM(tiles[1:], jnp.bfloat16)] * (chunks - early),
                *([pltpu.VMEM(part_tiles, jnp.float32)] if early else []),
            ],
            compiler_params=pltpu.CompilerParams(collective_id=0, has_side_effects=True),
            name="harvest",
        )(residuals, owners)
        return pl.pallas_call(
            store_kernel,
            out_shape=jax.ShapeDtypeStruct(received.shape, received.dtype),
            in_specs=[pl.BlockSpec(memory_space=pltpu.VMEM)],
            out_specs=pl.BlockSpec(memory_space=pl.ANY),
            scratch_shapes=[pltpu.SemaphoreType.DMA],
            name="store",
        )(pltpu.with_memory_space_constraint(received, pltpu.VMEM))

    in_specs = (P("section", "dp", None), P())
    out_specs = P(("section", "dp"), None, None)
    return jax.shard_map(on_device, mesh=mesh, in_specs=in_specs, out_specs=out_specs, check_vma=False)
```

profile of v0, /device:TPU:0, one launch (start us, length us, event | category | flops | bytes accessed | tf_op | source)
XLA Modules:
  0.0 22.9 jit_solution(2414268341785811284)
XLA Ops:
  0.0 22.2 %harvest.1.assembled = bf16[4,8,4096]{2,1,0:T(8,128)(2,1)S(1)} custom-call(f32[4,8,4096]{2,1,0:T(8,128)} %x_hbm.1, s32[32]{0:T(128)} %owners_hbm.1), custom_call_target="tpu_custom_call" | custom-call | tf_op jit(solution)/shard_map/harvest/pallas_call | solution.py:223
  22.2 0.7 %store.1 = bf16[4,8,4096]{2,1,0:T(8,128)(2,1)} custom-call(bf16[4,8,4096]{2,1,0:T(8,128)(2,1)S(1)} %harvest.1.assembled), custom_call_target="tpu_custom_call" | custom-call | tf_op jit(solution)/shard_map/store/pallas_call | solution.py:248
where the time goes:
time: 23.1 us; the launch traced here: 22.9 us
  Pallas kernels  22.9 us (99%)
    pallas_call x1, Pallas kernels, on_device(): pl.pallas_call(functools.partial(harvest_kernel, sections, groups, early)...  22.2 us
    pallas_call x1, Pallas kernels, on_device(): pl.pallas_call(store_kernel, out_shape=jax.ShapeDtypeStruct(received.shap...  0.71 us

commit v1 on v0

v1 whole, which is shorter than its diff:
```python
import functools

import jax
import jax.numpy as jnp
from jax import lax
from jax.experimental import pallas as pl
from jax.experimental.pallas import tpu as pltpu
from jax.sharding import PartitionSpec as P

MESH = pl.DeviceIdType.MESH
LANES = 128
SUBLANES = 8
QUARTERS = 4
EARLY = 2
LAG = 8


def harvest_kernel(sections, groups, planes, units, early, x_hbm, owners_hbm, out_ref, owners, inverse, xv, centered,
                   part, part2, parts, s1, s2, r2, x_sem, o_sem, e_send, e_recv, r_recv, below, above, send1, recv1,
                   send2, recv2, *r1):
    layers, tokens, features = x_hbm.shape
    blocks = s2.shape[1]
    per_dev = blocks // groups
    chunks = features // groups // LANES
    width = features // groups
    plane = groups // planes
    section, group = lax.axis_index("section"), lax.axis_index("dp")
    me = section * groups + group
    z, place = group // plane, lax.rem(group, plane)

    load = pltpu.make_async_copy(x_hbm, xv, x_sem)
    load.start()
    load_owners = pltpu.make_async_copy(owners_hbm, owners, o_sem)
    load_owners.start()
    barrier = pltpu.get_barrier_semaphore()

    def at(t, k):
        return (z + t) * plane + lax.rem(place + k, plane)

    def when(t, body):
        if t == 0:
            body()
        elif t > 0:
            pl.when(z < planes - t)(body)
        else:
            pl.when(z >= -t)(body)

    def peers(t):
        return range(1 if t == 0 else 0, plane)

    near = [t for t in (0, 1, -1) if abs(t) < planes]
    for t in near:
        @functools.partial(when, t)
        def _():
            for k in peers(t):
                pl.semaphore_signal(barrier, inc=1, device_id=(section, at(t, k)), device_id_type=MESH)
    for k in range(1, sections):
        pl.semaphore_signal(barrier, inc=1, device_id=(lax.rem(section + k, sections), group), device_id_type=MESH)

    load.wait()
    per_tile = SUBLANES // layers
    lane = lax.broadcasted_iota(jnp.int32, (SUBLANES, LANES), 1)
    row = lax.broadcasted_iota(jnp.int32, (SUBLANES, LANES), 0)
    total = jnp.zeros((SUBLANES, LANES), jnp.float32)
    for l in range(layers):
        acc = jnp.zeros((SUBLANES, LANES), jnp.float32)
        for t in range(0, tokens, SUBLANES):
            x = xv[l, t:t + SUBLANES]
            c = x - jnp.sum(x, axis=1, keepdims=True) * (1.0 / features)
            xv[l, t:t + SUBLANES] = c
            sq = c * c
            for f in range(features // LANES):
                acc = acc + sq[:, f * LANES:(f + 1) * LANES]
        fold = LANES // 2
        while fold >= LANES // layers:
            acc = acc + pltpu.roll(acc, fold, 1)
            fold //= 2
        total = total + jnp.where(lane // (LANES // layers) == l, acc, 0.0)
    own_lanes = lane // (LANES // layers) == row % layers
    acc = jnp.sum(total, axis=0, keepdims=True)
    part[...] = acc
    parts[group] = acc
    if planes > 3:
        @pl.when(z >= planes - 1)
        def _():
            parts[0:plane] = jnp.zeros((plane, 1, LANES), jnp.float32)

    tiles = range(tokens // per_tile)
    tiles_per_block = tokens // per_dev // per_tile

    def regroup(g):
        j, tile = divmod(g, tiles_per_block)
        c = jnp.concatenate([xv[:, g * per_tile + i, :] for i in range(per_tile)], axis=0)
        for f in range(features // LANES):
            centered[tile, f, j] = c[:, f * LANES:(f + 1) * LANES]

    early_tiles = {tile for tile, _ in units[:early]}
    first = [g for g in tiles if g % tiles_per_block in early_tiles]
    for g in first:
        regroup(g)

    mine = pl.ds(group * per_dev, per_dev)

    def send_part(source, t):
        for k in peers(t):
            pltpu.make_async_remote_copy(
                src_ref=source, dst_ref=parts.at[group], send_sem=e_send,
                recv_sem=r_recv if t == 1 and k == 0 else e_recv,
                device_id=(section, at(t, k)), device_id_type=MESH).start()

    def energies(count, sem=None):
        span = parts.at[pl.ds(0, count)]
        return pltpu.make_async_remote_copy(
            src_ref=span, dst_ref=span, send_sem=e_send, recv_sem=e_recv if sem is None else sem,
            device_id=(section, group), device_id_type=MESH)

    def relayed():
        return energies(1, r_recv)

    def send_unit(u, d, source):
        pltpu.make_async_remote_copy(
            src_ref=source, dst_ref=r1[u].at[mine], send_sem=send1.at[u], recv_sem=recv1.at[u],
            device_id=(section, d), device_id_type=MESH).start()

    def raw(u, d):
        tile, k = units[u]
        return centered.at[tile, d * chunks + k]

    def send_early(t):
        for u in range(early):
            for k in peers(t):
                send_unit(u, at(t, k), raw(u, at(t, k)))

    def neighbour(sem, t):
        pl.semaphore_signal(sem, inc=1, device_id=(section, at(t, 0)), device_id_type=MESH)

    both = (z + planes - 1) // planes + (2 * planes - 2 - z) // planes
    pl.semaphore_wait(barrier, plane * (1 + both) - 1 + sections - 1)
    for t in near:
        when(t, lambda: send_part(part, t))
    if planes > 2:
        @pl.when((z >= 1) & (z < planes - 1))
        def _():
            neighbour(below.at[2], 1)
            neighbour(above.at[2], -1)

    for t in range(2, planes):
        @functools.partial(when, -t)
        def _():
            pl.semaphore_wait(below.at[t], 1)
            if t + 1 < planes:
                when(1, lambda: neighbour(below.at[t + 1], 1))
            send_part(part, -t)

    for t in sorted([t for t in near if t] + [-t for t in range(2, planes)]):
        when(t, lambda: send_early(t))
    for t in range(2, planes):
        @functools.partial(when, t)
        def _():
            pl.semaphore_wait(above.at[t], 1)
            if t + 1 < planes:
                when(-1, lambda: neighbour(above.at[t + 1], -1))
            if t == 2:
                @pl.when(z >= 1)
                def _():
                    relayed().wait_recv()
                    part2[...] = part[...] + parts[group - plane]

                @pl.when(z < 1)
                def _():
                    part2[...] = part[...]
                send_part(part2, t)
            send_early(t)
    send_early(0)

    for g in tiles:
        if g not in first:
            regroup(g)
    load_owners.wait()

    @pl.loop(0, blocks)
    def _(o):
        found = jnp.int32(0)
        for b in range(blocks):
            found = jnp.where(owners[b] == o, jnp.int32(b), found)
        inverse[o] = found

    @pl.when(z < 1)
    def _():
        energies(groups - 1).wait_recv()

    @pl.when(z >= 1)
    def _():
        if planes <= 3:
            energies(groups - 2).wait_recv()
        else:
            @pl.when(z < planes - 1)
            def _():
                energies(groups - 2).wait_recv()

            @pl.when(z >= planes - 1)
            def _():
                energies(groups - 2 - plane).wait_recv()
        pl.when(z >= planes - 2)(lambda: relayed().wait_recv())

    total = parts[0]
    for g in range(1, groups):
        total = total + parts[g]
    energy = jnp.sum(jnp.where(own_lanes, total, 0.0), axis=1, keepdims=True)
    scale = 1.0 / jnp.sqrt(energy * (1.0 / (tokens * groups * features)) + 1.0)

    maps = [z]
    if planes > 1:
        half = lax.rem(z + 2, planes)
        maps = [planes - 1 - z, half, planes - 1 - half, z]

    def partners(m):
        return [maps[m] * plane + lax.rem(place + k, plane) for k in range(plane)]

    for u in range(early, len(units)):
        tile, k = units[u]
        for d in range(groups):
            for j in range(per_dev):
                s1[u - early, d * per_dev + j] = (centered[tile, d * chunks + k, j] * scale).astype(jnp.bfloat16)
        for m in range(len(maps)):
            for n, d in enumerate(partners(m)):
                if m < len(maps) - 1 or n:
                    send_unit(u, d, s1.at[u - early, pl.ds(d * per_dev, per_dev)])
        r1[u][mine] = s1[u - early, mine]
    for u in range(early):
        r1[u][mine] = raw(u, group)[...]

    def arrived(u):
        span = r1[u].at[pl.ds(0, (groups - 1) * per_dev)]
        return pltpu.make_async_remote_copy(
            src_ref=span, dst_ref=span, send_sem=send1.at[u], recv_sem=recv1.at[u],
            device_id=(section, group), device_id_type=MESH)

    def delivered(u):
        span = r2.at[u, pl.ds(0, sections * groups - 1)]
        return pltpu.make_async_remote_copy(
            src_ref=span, dst_ref=span, send_sem=send2.at[u], recv_sem=recv2.at[u],
            device_id=(section, group), device_id_type=MESH)

    routes = [(m, n, q) for m in range(len(maps)) for n in range(plane) for q in range(sections)]
    routes = [r for r in routes if r != (len(maps) - 1, 0, 0)] + [(len(maps) - 1, 0, 0)]

    def deliver(u):
        def spot(m, n, q):
            sec, d = lax.rem(section + q, sections), partners(m)[n]
            return sec, d, sec * groups + d

        def select(m, n, q):
            o = spot(m, n, q)[2]
            block = r1[u][inverse[o]]
            if u < early:
                block = (block * scale).astype(jnp.bfloat16)
            if (m, n, q) == routes[-1]:
                r2[u, o] = block
            else:
                s2[u, o] = block

        def send(m, n, q):
            sec, d, o = spot(m, n, q)
            pltpu.make_async_remote_copy(
                src_ref=s2.at[u, o], dst_ref=r2.at[u, me], send_sem=send2.at[u], recv_sem=recv2.at[u],
                device_id=(sec, d), device_id_type=MESH).start()

        for n in range(len(routes) + LAG):
            if n < len(routes):
                select(*routes[n])
            if LAG <= n < len(routes) - 1 + LAG:
                send(*routes[n - LAG])

    for u in range(len(units)):
        arrived(u).wait_recv()
        deliver(u)

    for u, (tile, k) in enumerate(units):
        delivered(u).wait_recv()
        for d in range(groups):
            got = [r2[u, s * groups + d].astype(jnp.float32) for s in range(sections)]
            lane = d * width + k * LANES
            for i in range(per_tile):
                out_ref[tile * per_tile + i, :, lane:lane + LANES] = jnp.concatenate(
                    [v[i * layers:(i + 1) * layers] for v in got], axis=0).astype(jnp.bfloat16)

    if planes > 3:
        @pl.when(z < 1)
        def _():
            energies(groups - 1 - plane).wait_send()

        @pl.when(z >= 1)
        def _():
            energies(groups - 1).wait_send()
    else:
        energies(groups - 1).wait_send()
    for u in range(len(units)):
        arrived(u).wait_send()
        delivered(u).wait_send()


def store_kernel(assembled, out_hbm, sem):
    store = pltpu.make_async_copy(assembled, out_hbm, sem)
    store.start()
    store.wait()


def solution(mesh):
    sections, groups = mesh.shape["section"], mesh.shape["dp"]
    planes = QUARTERS if groups % QUARTERS == 0 else 1

    def on_device(residuals, owners):
        layers, tokens, features = residuals.shape
        blocks = owners.shape[0]
        per_dev = blocks // groups
        block_len = tokens // per_dev
        chunks = features // groups // LANES
        row_tiles = block_len * layers // SUBLANES
        units = [(tile, k) for tile in range(row_tiles) for k in range(chunks)]
        early = min(EARLY, len(units) // 2)
        tile = (SUBLANES, LANES)
        dma, flag = pltpu.SemaphoreType.DMA, pltpu.SemaphoreType.REGULAR
        received = pl.pallas_call(
            functools.partial(harvest_kernel, sections, groups, planes, units, early),
            out_shape=pltpu.VMEM((block_len, layers * sections, features), jnp.bfloat16),
            in_specs=[pl.BlockSpec(memory_space=pl.ANY), pl.BlockSpec(memory_space=pl.ANY)],
            out_specs=pl.BlockSpec(memory_space=pltpu.VMEM),
            scratch_shapes=[
                pltpu.SMEM((blocks,), jnp.int32),
                pltpu.SMEM((blocks,), jnp.int32),
                pltpu.VMEM((layers, tokens, features), jnp.float32),
                pltpu.VMEM((row_tiles, features // LANES, per_dev, *tile), jnp.float32),
                pltpu.VMEM((1, LANES), jnp.float32),
                pltpu.VMEM((1, LANES), jnp.float32),
                pltpu.VMEM((groups, 1, LANES), jnp.float32),
                pltpu.VMEM((len(units) - early, blocks, *tile), jnp.bfloat16),
                pltpu.VMEM((len(units), blocks, *tile), jnp.bfloat16),
                pltpu.VMEM((len(units), blocks, *tile), jnp.bfloat16),
                dma, dma, dma, dma, dma,
                flag((QUARTERS,)), flag((QUARTERS,)),
                *[dma((len(units),)) for _ in range(4)],
                *[pltpu.VMEM((blocks, *tile), jnp.float32 if u < early else jnp.bfloat16) for u in range(len(units))],
            ],
            compiler_params=pltpu.CompilerParams(collective_id=0, has_side_effects=True),
            name="harvest",
        )(residuals, owners)
        return pl.pallas_call(
            store_kernel,
            out_shape=jax.ShapeDtypeStruct(received.shape, received.dtype),
            in_specs=[pl.BlockSpec(memory_space=pltpu.VMEM)],
            out_specs=pl.BlockSpec(memory_space=pl.ANY),
            scratch_shapes=[pltpu.SemaphoreType.DMA],
            name="store",
        )(pltpu.with_memory_space_constraint(received, pltpu.VMEM))

    in_specs = (P("section", "dp", None), P())
    out_specs = P(("section", "dp"), None, None)
    return jax.shard_map(on_device, mesh=mesh, in_specs=in_specs, out_specs=out_specs, check_vma=False)
```

time: 23.1 us -> 24.3 us (1.052)
  Pallas kernels: 22.9 us -> 24.1 us
    pallas_call x1, Pallas kernels: 22.2 us -> 23.4 us  [on_device(): pl.pallas_call(functools.partial(harvest_kernel, sections, groups, planes...]
where the time goes in v1:
time: 24.3 us; the launch traced here: 24.1 us
  Pallas kernels  24.1 us (99%)
    pallas_call x1, Pallas kernels, on_device(): pl.pallas_call(functools.partial(harvest_kernel, sections, groups, planes...  23.4 us
    pallas_call x1, Pallas kernels, on_device(): pl.pallas_call(store_kernel, out_shape=jax.ShapeDtypeStruct(received.shap...  0.71 us

profile of v1, /device:TPU:0, one launch (start us, length us, event | category | flops | bytes accessed | tf_op | source)
XLA Modules:
  0.0 24.1 jit_solution(2893787066114529781)
XLA Ops:
  0.0 23.4 %harvest.1.assembled = bf16[4,8,4096]{2,1,0:T(8,128)(2,1)S(1)} custom-call(f32[4,8,4096]{2,1,0:T(8,128)} %x_hbm.1, s32[32]{0:T(128)} %owners_hbm.1), custom_call_target="tpu_custom_call" | custom-call | tf_op jit(solution)/shard_map/harvest/pallas_call | solution.py:324
  23.4 0.7 %store.1 = bf16[4,8,4096]{2,1,0:T(8,128)(2,1)} custom-call(bf16[4,8,4096]{2,1,0:T(8,128)(2,1)S(1)} %harvest.1.assembled), custom_call_target="tpu_custom_call" | custom-call | tf_op jit(solution)/shard_map/store/pallas_call | solution.py:348

commit v2 on v0

v2 whole, which is shorter than its diff:
```python
import functools

import jax
import jax.numpy as jnp
from jax import lax
from jax.experimental import pallas as pl
from jax.experimental.pallas import tpu as pltpu
from jax.sharding import PartitionSpec as P

MESH = pl.DeviceIdType.MESH
LANES = 128
SUBLANES = 8
LAG = 8
FULL = 1
EFIRST = 1
SPLIT = 0
LSPLIT = 0
NUNITS = 3
ORDE = 'near'
ORDL = 'near'
STEPS = ((0, (0, 2)), (1, (0, 2, 3)), (2, (0, 2, 3)), (0, (1, 3)), (1, (1,)), (2, (1,)))


def harvest_kernel(sections, groups, narrow, kinds, x_hbm, owners_hbm, out_ref, owners, inverse, xv, centered, part,
                   parts, x_sem, o_sem, e_send, e_recv, send1, recv1, send2, recv2, *buffers):
    layers, tokens, features = x_hbm.shape
    pieces = features // LANES
    blocks = owners.shape[0]
    per_dev = blocks // groups
    side, quarter = groups // 2, groups // 4
    row_tiles = centered.shape[0]
    each = sum(len(k) for k in kinds)
    wide_chunks = groups * each // row_tiles
    units = narrow + len(kinds)
    r1, s2, r2, late = buffers[:units], buffers[units:2 * units], buffers[2 * units:3 * units], buffers[3 * units:]
    section, group = lax.axis_index("section"), lax.axis_index("dp")
    me = section * groups + group
    upper = group // side
    spot, base = lax.rem(group, side), upper * side

    load = pltpu.make_async_copy(x_hbm, xv, x_sem)
    load.start()
    load_owners = pltpu.make_async_copy(owners_hbm, owners, o_sem)
    load_owners.start()
    barrier = pltpu.get_barrier_semaphore()

    def peer_of(p):
        return lax.rem(group + p, groups)

    def beside(k):
        return base + lax.rem(spot + k, side)

    def across(k):
        return side - base + lax.rem(spot + k, side)

    def signal(sem, d):
        pl.semaphore_signal(sem, inc=1, device_id=(section, d), device_id_type=MESH)

    for p in range(1, groups):
        signal(barrier, peer_of(p))
    for k in range(1, sections):
        pl.semaphore_signal(barrier, inc=1, device_id=(lax.rem(section + k, sections), group), device_id_type=MESH)

    load.wait()
    per_tile = SUBLANES // layers
    lane = lax.broadcasted_iota(jnp.int32, (SUBLANES, LANES), 1)
    row = lax.broadcasted_iota(jnp.int32, (SUBLANES, LANES), 0)
    total = jnp.zeros((SUBLANES, LANES), jnp.float32)
    for l in range(layers):
        acc = jnp.zeros((SUBLANES, LANES), jnp.float32)
        for t in range(0, tokens, SUBLANES):
            x = xv[l, t:t + SUBLANES]
            c = x - jnp.sum(x, axis=1, keepdims=True) * (1.0 / features)
            xv[l, t:t + SUBLANES] = c
            sq = c * c
            for f in range(pieces):
                acc = acc + sq[:, f * LANES:(f + 1) * LANES]
        fold = LANES // 2
        while fold >= LANES // layers:
            acc = acc + pltpu.roll(acc, fold, 1)
            fold //= 2
        total = total + jnp.where(lane // (LANES // layers) == l, acc, 0.0)
    own_lanes = lane // (LANES // layers) == row % layers
    acc = jnp.sum(total, axis=0, keepdims=True)
    part[...] = acc
    parts[group] = acc

    for g in range(tokens // per_tile):
        j, tile = divmod(g, row_tiles)
        c = jnp.concatenate([xv[:, g * per_tile + i, :] for i in range(per_tile)], axis=0)
        for f in range(pieces):
            centered[tile, f, j] = c[:, f * LANES:(f + 1) * LANES]

    def send_part(source, d, sem):
        pltpu.make_async_remote_copy(
            src_ref=source, dst_ref=parts.at[group], send_sem=e_send, recv_sem=sem,
            device_id=(section, d), device_id_type=MESH).start()

    def energies(count, sem):
        span = parts.at[pl.ds(0, count)]
        return pltpu.make_async_remote_copy(
            src_ref=span, dst_ref=span, send_sem=e_send, recv_sem=sem,
            device_id=(section, group), device_id_type=MESH)

    def source(u, d):
        if u < narrow:
            return centered.at[:, wide_chunks + lax.rem(d, side) * narrow + u]
        if u > narrow:
            return late[u - narrow - 1].at[:, pl.ds(d * per_dev, per_dev)]
        piece = d * each
        return centered.at[pl.ds(lax.rem(piece, row_tiles), 1), piece // row_tiles]

    def slot(u):
        return pl.ds((spot if u < narrow else group) * per_dev, per_dev)

    def spread(u, d):
        pltpu.make_async_remote_copy(
            src_ref=source(u, d), dst_ref=r1[u].at[:, slot(u)], send_sem=send1.at[u], recv_sem=recv1.at[u],
            device_id=(section, d), device_id_type=MESH).start()

    def circle(kind):
        if kind == 'near':
            return [peer_of(p) for p in sorted(range(1, groups), key=lambda p: min(p, groups - p))]
        if kind == 'rot':
            return [peer_of(p) for p in range(1, groups)]
        return [across(k) for k in range(side)] + [beside(k) for k in range(1, side)]

    pl.semaphore_wait(barrier, groups + sections - 2)
    for d in circle('near'):
        send_part(part, d, e_recv)
    if EFIRST == 1:
        for d in circle(ORDE):
            spread(narrow, d)
    elif EFIRST == 2:
        for k in range(side):
            spread(narrow, across(k))
    for u in range(narrow):
        for k in range(1, side):
            spread(u, beside(k))
        if EFIRST == 2 and u == 0:
            for k in range(1, side):
                spread(narrow, beside(k))

    load_owners.wait()

    @pl.loop(0, blocks)
    def _(o):
        found = jnp.int32(0)
        for b in range(blocks):
            found = jnp.where(owners[b] == o, jnp.int32(b), found)
        inverse[o] = found

    for u in range(narrow + 1):
        r1[u][:, slot(u)] = source(u, group)[...]
    energies(groups - 1, e_recv).wait_recv()
    total = parts[0]
    for g in range(1, groups):
        total = total + parts[g]
    energy = jnp.sum(jnp.where(own_lanes, total, 0.0), axis=1, keepdims=True)
    scale = 1.0 / jnp.sqrt(energy * (1.0 / (tokens * groups * features)) + 1.0)

    for u in range(narrow + 1, units):
        for n, i in enumerate(kinds[u - narrow]):
            for d in range(groups):
                chunk, tile = divmod(d * each + i, row_tiles)
                for j in range(per_dev):
                    late[u - narrow - 1][n, d * per_dev + j] = (centered[tile, chunk, j] * scale).astype(jnp.bfloat16)
        for d in circle(ORDL):
            spread(u, d)
        r1[u][:, slot(u)] = late[u - narrow - 1][:, slot(u)]

    def arrived(u):
        span = r1[u].at[:, pl.ds(0, ((side if u < narrow else groups) - 1) * per_dev)]
        return pltpu.make_async_remote_copy(
            src_ref=span, dst_ref=span, send_sem=send1.at[u], recv_sem=recv1.at[u],
            device_id=(section, group), device_id_type=MESH)

    def delivered(u):
        span = r2[u].at[pl.ds(0, sections * groups - 1)]
        return pltpu.make_async_remote_copy(
            src_ref=span, dst_ref=span, send_sem=send2.at[u], recv_sem=recv2.at[u],
            device_id=(section, group), device_id_type=MESH)

    plane, corner = group // quarter, lax.rem(group, quarter)

    def take(u, o):
        b = inverse[o]
        if u < narrow:
            b = lax.rem(b, side * per_dev)
        got = [r1[u][tile, b] for tile in range(r1[u].shape[0])]
        return [(v * scale).astype(jnp.bfloat16) for v in got] if u <= narrow else got

    def deliver(u, planes):
        if SPLIT:
            routes = [(t, k, q) for k in range(quarter) for q in range(sections) for t in planes]
        else:
            routes = [(t, k, q) for t in planes for k in range(quarter) for q in range(sections)]

        def place(t, k, q):
            sec, d = lax.rem(section + q, sections), t * quarter + lax.rem(corner + k, quarter)
            return sec, d, sec * groups + d

        def select(t, k, q):
            o = place(t, k, q)[2]
            for tile, block in enumerate(take(u, o)):
                s2[u][o, tile] = block

        def send(t, k, q):
            sec, d, o = place(t, k, q)

            def go():
                pltpu.make_async_remote_copy(
                    src_ref=s2[u].at[o], dst_ref=r2[u].at[me], send_sem=send2.at[u], recv_sem=recv2.at[u],
                    device_id=(sec, d), device_id_type=MESH).start()
            if k or q:
                go()
            else:
                pl.when(plane != t)(go)

        for n in range(len(routes) + LAG):
            if n < len(routes):
                select(*routes[n])
            if n >= LAG:
                send(*routes[n - LAG])

    steps = STEPS if units == NUNITS else [(u, (0, 1, 2, 3)) for u in range(units)]
    seen = []
    for u, planes in steps:
        if u not in seen:
            arrived(u).wait_recv()
            seen.append(u)
        deliver(u, planes)
    for u in seen:
        for tile, block in enumerate(take(u, me)):
            r2[u][me, tile] = block
    order = seen

    home = inverse[me] // (side * per_dev) * side

    def assemble(tile, chunk, got):
        for i in range(per_tile):
            out_ref[tile * per_tile + i, :, chunk * LANES:(chunk + 1) * LANES] = jnp.concatenate(
                [v[i * layers:(i + 1) * layers] for v in got], axis=0).astype(jnp.bfloat16)

    for u in order:
        delivered(u).wait_recv()
        if u < narrow:
            for d in range(side):
                for tile in range(row_tiles):
                    assemble(tile, wide_chunks + d * narrow + u,
                             [r2[u][s * groups + home + d, tile].astype(jnp.float32) for s in range(sections)])
        else:
            for d in range(groups):
                for n, i in enumerate(kinds[u - narrow]):
                    chunk, tile = divmod(d * each + i, row_tiles)
                    assemble(tile, chunk, [r2[u][s * groups + d, n].astype(jnp.float32) for s in range(sections)])

    energies(groups - 1, e_recv).wait_send()
    for u in range(units):
        arrived(u).wait_send()
        delivered(u).wait_send()


def store_kernel(assembled, out_hbm, sem):
    store = pltpu.make_async_copy(assembled, out_hbm, sem)
    store.start()
    store.wait()


def solution(mesh):
    sections, groups = mesh.shape["section"], mesh.shape["dp"]

    def on_device(residuals, owners):
        layers, tokens, features = residuals.shape
        blocks = owners.shape[0]
        per_dev = blocks // groups
        block_len = tokens // per_dev
        row_tiles = block_len * layers // SUBLANES
        pieces, side = features // LANES * row_tiles, groups // 2
        narrow = 1
        each = (pieces - narrow * row_tiles * side) // groups
        if LSPLIT:
            kinds = [[i] for i in range(each)]
        else:
            kinds = [[0]] + ([list(range(1, each))] if each > 1 else [])
        units = narrow + len(kinds)
        tile = (SUBLANES, LANES)
        dma = pltpu.SemaphoreType.DMA
        tiles_of = [row_tiles] * narrow + [len(k) for k in kinds]
        received = pl.pallas_call(
            functools.partial(harvest_kernel, sections, groups, narrow, kinds),
            out_shape=pltpu.VMEM((block_len, layers * sections, features), jnp.bfloat16),
            in_specs=[pl.BlockSpec(memory_space=pl.ANY), pl.BlockSpec(memory_space=pl.ANY)],
            out_specs=pl.BlockSpec(memory_space=pltpu.VMEM),
            scratch_shapes=[
                pltpu.SMEM((blocks,), jnp.int32),
                pltpu.SMEM((blocks,), jnp.int32),
                pltpu.VMEM((layers, tokens, features), jnp.float32),
                pltpu.VMEM((row_tiles, features // LANES, per_dev, *tile), jnp.float32),
                pltpu.VMEM((1, LANES), jnp.float32),
                pltpu.VMEM((groups, 1, LANES), jnp.float32),
                dma, dma, dma, dma,
                *[dma((units,)) for _ in range(4)],
                *[pltpu.VMEM((tiles_of[u], blocks // (2 if u < narrow else 1), *tile),
                             jnp.float32 if u <= narrow else jnp.bfloat16) for u in range(units)],
                *[pltpu.VMEM((blocks, tiles_of[u], *tile), jnp.bfloat16) for u in range(units)] * 2,
                *[pltpu.VMEM((len(k), blocks, *tile), jnp.bfloat16) for k in kinds[1:]],
            ],
            compiler_params=pltpu.CompilerParams(collective_id=0, has_side_effects=True),
            name="harvest",
        )(residuals, owners)
        return pl.pallas_call(
            store_kernel,
            out_shape=jax.ShapeDtypeStruct(received.shape, received.dtype),
            in_specs=[pl.BlockSpec(memory_space=pltpu.VMEM)],
            out_specs=pl.BlockSpec(memory_space=pl.ANY),
            scratch_shapes=[pltpu.SemaphoreType.DMA],
            name="store",
        )(pltpu.with_memory_space_constraint(received, pltpu.VMEM))

    in_specs = (P("section", "dp", None), P())
    out_specs = P(("section", "dp"), None, None)
    return jax.shard_map(on_device, mesh=mesh, in_specs=in_specs, out_specs=out_specs, check_vma=False)
```

time: 23.1 us -> 22.3 us (0.965)
  the two profiles are of different devices: /device:TPU:0 before, /device:TPU:1 now
where the time goes in v2:
time: 22.3 us; the launch traced here: 22.2 us
  Pallas kernels  22.2 us (100%)
    pallas_call x1, Pallas kernels, on_device(): pl.pallas_call(functools.partial(harvest_kernel, sections, groups, narrow...  21.5 us
    pallas_call x1, Pallas kernels, on_device(): pl.pallas_call(store_kernel, out_shape=jax.ShapeDtypeStruct(received.shap...  0.71 us

profile of v2, /device:TPU:1, one launch (start us, length us, event | category | flops | bytes accessed | tf_op | source)
XLA Modules:
  0.0 22.2 jit_solution(5869040761968572718)
XLA Ops:
  0.0 21.5 %harvest.1.assembled = bf16[4,8,4096]{2,1,0:T(8,128)(2,1)S(1)} custom-call(f32[4,8,4096]{2,1,0:T(8,128)} %x_hbm.1, s32[32]{0:T(128)} %owners_hbm.1), custom_call_target="tpu_custom_call" | custom-call | tf_op jit(solution)/shard_map/harvest/pallas_call | solution.py:290
  21.5 0.7 %store.1 = bf16[4,8,4096]{2,1,0:T(8,128)(2,1)} custom-call(bf16[4,8,4096]{2,1,0:T(8,128)(2,1)S(1)} %harvest.1.assembled), custom_call_target="tpu_custom_call" | custom-call | tf_op jit(solution)/shard_map/store/pallas_call | solution.py:312

commit v3 on v2

v3 whole, which is shorter than its diff:
```python
import functools

import jax
import jax.numpy as jnp
from jax import lax
from jax.experimental import pallas as pl
from jax.experimental.pallas import tpu as pltpu
from jax.sharding import PartitionSpec as P

MESH = pl.DeviceIdType.MESH
LANES = 128
SUBLANES = 8
LAG = 8
SHARE = 0
JOINED = 1
LI = 1
ABS = 2
STAGED = 0
LOW = (0, 1, 2)
ORDL = 'near'
ORDE = 'near'
PRE = ((1,), (0,), (2,))
STEPS = ((0, (0, 2)), (1, (0, 2, 3)), (0, ((1, 'a'), 3)), (2, (0, 2, 3)), (1, ((1, 'a'),)), (2, ((1, 'a'),)),
         (0, ((1, 'b'),)), (1, ((1, 'b'),)), (2, ((1, 'b'),)))


def layout(row_tiles, per_dev, each):
    share = per_dev // SHARE if SHARE else 0
    boxes = [(True, None, 0, per_dev, True), (False, 0, 0, per_dev, True)]
    units = [[0], [1]]
    rest = []
    for piece in range(1, each):
        cut = share if piece == 1 else 0
        if cut:
            boxes.append((False, piece, 0, cut, True))
        boxes.append((False, piece, cut, per_dev, False))
        rest.append(piece)
    units += [rest] if JOINED and rest else [[p] for p in rest]
    return boxes, units


def harvest_kernel(sections, groups, each, x_hbm, owners_hbm, out_ref, owners, inverse, xv, centered, part,
                   parts, x_sem, o_sem, e_send, e_recv, ready, send1, recv1, send2, recv2, *buffers):
    layers, tokens, features = x_hbm.shape
    pieces = features // LANES
    blocks = owners.shape[0]
    per_dev = blocks // groups
    side, quarter = groups // 2, groups // 4
    row_tiles = centered.shape[0]
    wide_chunks = groups * each // row_tiles
    boxes, units = layout(row_tiles, per_dev, each)
    nb, nu = len(boxes), len(units)
    r1, s2, r2, late = buffers[:nb], buffers[nb:nb + nu], buffers[nb + nu:nb + 2 * nu], buffers[nb + 2 * nu:]
    late = dict(zip([b for b in range(nb) if not boxes[b][4]], late))
    section, group = lax.axis_index("section"), lax.axis_index("dp")
    me = section * groups + group
    upper = group // side
    spot, base = lax.rem(group, side), upper * side

    load = pltpu.make_async_copy(x_hbm, xv, x_sem)
    load.start()
    load_owners = pltpu.make_async_copy(owners_hbm, owners, o_sem)
    load_owners.start()
    barrier = pltpu.get_barrier_semaphore()

    def peer_of(p):
        return lax.rem(group + p, groups)

    def beside(k):
        return base + lax.rem(spot + k, side)

    def across(k):
        return side - base + lax.rem(spot + k, side)

    def signal(sem, d):
        pl.semaphore_signal(sem, inc=1, device_id=(section, d), device_id_type=MESH)

    plane, corner = group // quarter, lax.rem(group, quarter)

    def member(t, k):
        return t * quarter + lax.rem(corner + k, quarter)

    for t in range(4):
        for k in range(quarter):
            if t == 0 and STAGED:
                pl.when((plane == 1) | (plane == 0) if k else plane == 1)(lambda: signal(barrier, member(t, k)))
            elif k:
                signal(barrier, member(t, k))
            else:
                pl.when(plane != t)(lambda: signal(barrier, member(t, k)))
    for k in range(1, sections):
        pl.semaphore_signal(barrier, inc=1, device_id=(lax.rem(section + k, sections), group), device_id_type=MESH)

    load.wait()
    per_tile = SUBLANES // layers
    lane = lax.broadcasted_iota(jnp.int32, (SUBLANES, LANES), 1)
    row = lax.broadcasted_iota(jnp.int32, (SUBLANES, LANES), 0)
    total = jnp.zeros((SUBLANES, LANES), jnp.float32)
    for l in range(layers):
        acc = jnp.zeros((SUBLANES, LANES), jnp.float32)
        for t in range(0, tokens, SUBLANES):
            x = xv[l, t:t + SUBLANES]
            c = x - jnp.sum(x, axis=1, keepdims=True) * (1.0 / features)
            xv[l, t:t + SUBLANES] = c
            sq = c * c
            for f in range(pieces):
                acc = acc + sq[:, f * LANES:(f + 1) * LANES]
        fold = LANES // 2
        while fold >= LANES // layers:
            acc = acc + pltpu.roll(acc, fold, 1)
            fold //= 2
        total = total + jnp.where(lane // (LANES // layers) == l, acc, 0.0)
    own_lanes = lane // (LANES // layers) == row % layers
    acc = jnp.sum(total, axis=0, keepdims=True)
    part[...] = acc
    parts[group] = acc

    for g in range(tokens // per_tile):
        j, tile = divmod(g, row_tiles)
        c = jnp.concatenate([xv[:, g * per_tile + i, :] for i in range(per_tile)], axis=0)
        for f in range(pieces):
            centered[tile, f, j] = c[:, f * LANES:(f + 1) * LANES]

    def send_part(source, d, sem):
        pltpu.make_async_remote_copy(
            src_ref=source, dst_ref=parts.at[group], send_sem=e_send, recv_sem=sem,
            device_id=(section, d), device_id_type=MESH).start()

    def energies(count, sem):
        span = parts.at[pl.ds(0, count)]
        return pltpu.make_async_remote_copy(
            src_ref=span, dst_ref=span, send_sem=e_send, recv_sem=sem,
            device_id=(section, group), device_id_type=MESH)

    def source(b, d):
        half, piece, low, high, raw = boxes[b]
        if half:
            return centered.at[:, wide_chunks + lax.rem(d, side)]
        if not raw:
            return late[b].at[:, pl.ds(d * (high - low), high - low)]
        at = d * each + piece
        return centered.at[pl.ds(lax.rem(at, row_tiles), 1), at // row_tiles, pl.ds(low, high - low)]

    def slot(b):
        half, _, low, high, _ = boxes[b]
        return pl.ds((spot if half else group) * (high - low), high - low)

    def spread(*group_of, peers=None):
        first = group_of[0]
        if peers is None:
            peers = [beside(k) for k in range(1, side)] if boxes[first][0] else circle(ORDE if boxes[first][4] else ORDL)
        for d, b in [(d, b) for d in peers for b in group_of]:
            pltpu.make_async_remote_copy(
                src_ref=source(b, d), dst_ref=r1[b].at[:, slot(b)], send_sem=send1.at[b], recv_sem=recv1.at[b],
                device_id=(section, d), device_id_type=MESH).start()

    def circle(kind):
        if kind == 'near':
            return [peer_of(p) for p in sorted(range(1, groups), key=lambda p: min(p, groups - p))]
        if kind == 'rot':
            return [peer_of(p) for p in range(1, groups)]
        return [across(k) for k in range(side)] + [beside(k) for k in range(1, side)]

    early = [b for b in range(nb) if boxes[b][4]]

    def full_start():
        for d in circle('near'):
            send_part(part, d, e_recv)
        for bs in PRE:
            bs = [b for b in bs if b in early]
            if bs:
                spread(*bs)

    if STAGED:
        some = (plane + 3) // 4
        pl.semaphore_wait(barrier, side - 1 + sections - 1 + side * some)

        @pl.when(plane == 0)
        def _():
            nearby = [beside(k) for k in range(1, side)]
            distant = [across(k) for k in range(side)]
            for d in nearby:
                send_part(part, d, e_recv)
            for b in LOW:
                if b in early:
                    spread(b, peers=nearby)
            pl.semaphore_wait(ready, 1)
            for d in distant:
                send_part(part, d, e_recv)
            for b in LOW:
                if b in early and b:
                    spread(b, peers=distant)

        @pl.when(plane >= 1)
        def _():
            pl.when(plane == 1)(lambda: signal(ready, group - quarter))
            full_start()
    else:
        pl.semaphore_wait(barrier, groups + sections - 2)
        full_start()

    load_owners.wait()

    @pl.loop(0, blocks)
    def _(o):
        found = jnp.int32(0)
        for b in range(blocks):
            found = jnp.where(owners[b] == o, jnp.int32(b), found)
        inverse[o] = found

    for b in early:
        r1[b][:, slot(b)] = source(b, group)[...]
    energies(groups - 1, e_recv).wait_recv()
    total = parts[0]
    for g in range(1, groups):
        total = total + parts[g]
    energy = jnp.sum(jnp.where(own_lanes, total, 0.0), axis=1, keepdims=True)
    scale = 1.0 / jnp.sqrt(energy * (1.0 / (tokens * groups * features)) + 1.0)

    for b, out in late.items():
        _, piece, low, high, _ = boxes[b]
        for d in range(groups):
            chunk, tile = divmod(d * each + piece, row_tiles)
            for j in range(low, high):
                out[0, d * (high - low) + j - low] = (centered[tile, chunk, j] * scale).astype(jnp.bfloat16)
        if not LI:
            spread(b)
    if late and LI:
        spread(*late)
    for b, out in late.items():
        r1[b][:, slot(b)] = out[:, slot(b)]

    def arrived(b):
        half, _, low, high, _ = boxes[b]
        span = r1[b].at[:, pl.ds(0, ((side if half else groups) - 1) * (high - low))]
        return pltpu.make_async_remote_copy(
            src_ref=span, dst_ref=span, send_sem=send1.at[b], recv_sem=recv1.at[b],
            device_id=(section, group), device_id_type=MESH)

    def delivered(u):
        span = r2[u].at[pl.ds(0, sections * groups - 1)]
        return pltpu.make_async_remote_copy(
            src_ref=span, dst_ref=span, send_sem=send2.at[u], recv_sem=recv2.at[u],
            device_id=(section, group), device_id_type=MESH)

    def boxes_of(piece):
        return [b for b in range(nb) if boxes[b][1] == piece and not boxes[b][0]]

    def needs(u):
        return [0] if u == 0 else [b for piece in (units[u] if u > 1 else [0]) for b in boxes_of(piece)]

    def scaled(v):
        return (v * scale).astype(jnp.bfloat16)

    def take(u, o):
        at = inverse[o]
        if u == 0:
            at = lax.rem(at, side * per_dev)
            return [scaled(r1[0][tile, at]) for tile in range(row_tiles)]
        if u == 1:
            return [scaled(r1[1][0, at])]
        got = []
        for piece in units[u]:
            which = boxes_of(piece)
            if len(which) == 1:
                got.append(r1[which[0]][0, at])
            else:
                cut = boxes[which[0]][3]
                d, j = at // per_dev, lax.rem(at, per_dev)
                first = scaled(r1[which[0]][0, d * cut + lax.rem(j, cut)])
                second = r1[which[1]][0, d * (per_dev - cut) + lax.rem(j, per_dev - cut)]
                got.append(jnp.where(j < cut, first, second))
        return got

    def deliver(u, planes):
        if ABS == 1:
            keys = [(h, c, q) for q in range(sections) for h in range(quarter // 2) for c in range(2)]
        elif ABS == 2:
            keys = [(h, c, q) for h in range(quarter // 2) for q in range(sections) for c in range(2)]
        elif ABS == 3:
            keys = [(h, c, q) for h in range(quarter // 2) for c in range(2) for q in range(sections)]
        else:
            keys = [(h, c, q) for h in range(quarter // 2) for c in range(2) for q in range(sections)]
        routes = []
        for t in planes:
            t, part = t if isinstance(t, tuple) else (t, None)
            routes += [(t, k, k[2]) for k in keys if part is None or (part == 'a') == (k[0] == 0 and k[2] == 0)]

        def place(t, k, q):
            h, c, _ = k
            if ABS:
                sec, d = jnp.int32(q), t * quarter + h * 2 + lax.rem(corner + c, 2)
            else:
                sec, d = lax.rem(section + q, sections), t * quarter + lax.rem(corner + h * 2 + c, quarter)
            return sec, d, sec * groups + d

        def select(t, k, q):
            o = place(t, k, q)[2]
            for tile, block in enumerate(take(u, o)):
                s2[u][o, tile] = block

        def send(t, k, q):
            sec, d, o = place(t, k, q)

            def go():
                pltpu.make_async_remote_copy(
                    src_ref=s2[u].at[o], dst_ref=r2[u].at[me], send_sem=send2.at[u], recv_sem=recv2.at[u],
                    device_id=(sec, d), device_id_type=MESH).start()
            h, c, _ = k
            if ABS and not c:
                pl.when((plane != t) | (section != q) | (corner // 2 != h))(go)
            elif not ABS and not (h or c or q):
                pl.when(plane != t)(go)
            else:
                go()

        for n in range(len(routes) + LAG):
            if n < len(routes):
                select(*routes[n])
            if n >= LAG:
                send(*routes[n - LAG])

    steps = STEPS if nu == max(u for u, _ in STEPS) + 1 else [(u, (0, 1, 2, 3)) for u in range(nu)]
    seen = []
    for u, planes in steps:
        if u not in seen:
            for b in needs(u):
                arrived(b).wait_recv()
            seen.append(u)
        deliver(u, planes)
    for u in seen:
        for tile, block in enumerate(take(u, me)):
            r2[u][me, tile] = block
    order = seen

    home = inverse[me] // (side * per_dev) * side

    def assemble(tile, chunk, got):
        for i in range(per_tile):
            out_ref[tile * per_tile + i, :, chunk * LANES:(chunk + 1) * LANES] = jnp.concatenate(
                [v[i * layers:(i + 1) * layers] for v in got], axis=0).astype(jnp.bfloat16)

    for u in order:
        delivered(u).wait_recv()
        if u == 0:
            for d in range(side):
                for tile in range(row_tiles):
                    assemble(tile, wide_chunks + d,
                             [r2[u][s * groups + home + d, tile].astype(jnp.float32) for s in range(sections)])
        else:
            for d in range(groups):
                for n, piece in enumerate(units[u] if u > 1 else [0]):
                    chunk, tile = divmod(d * each + piece, row_tiles)
                    assemble(tile, chunk, [r2[u][s * groups + d, n].astype(jnp.float32) for s in range(sections)])

    energies(groups - 1, e_recv).wait_send()
    for b in range(nb):
        arrived(b).wait_send()
    for u in range(nu):
        delivered(u).wait_send()


def store_kernel(assembled, out_hbm, sem):
    store = pltpu.make_async_copy(assembled, out_hbm, sem)
    store.start()
    store.wait()


def solution(mesh):
    sections, groups = mesh.shape["section"], mesh.shape["dp"]

    def on_device(residuals, owners):
        layers, tokens, features = residuals.shape
        blocks = owners.shape[0]
        per_dev = blocks // groups
        block_len = tokens // per_dev
        row_tiles = block_len * layers // SUBLANES
        pieces, side = features // LANES * row_tiles, groups // 2
        each = (pieces - row_tiles * side) // groups
        boxes, units = layout(row_tiles, per_dev, each)
        tile = (SUBLANES, LANES)
        dma = pltpu.SemaphoreType.DMA
        inboxes = [(row_tiles if half else 1, (side if half else groups) * (high - low), *tile)
                   for half, _, low, high, _ in boxes]
        outboxes = [(blocks, row_tiles if u == 0 else 1 if u == 1 else len(units[u]), *tile) for u in range(len(units))]
        received = pl.pallas_call(
            functools.partial(harvest_kernel, sections, groups, each),
            out_shape=pltpu.VMEM((block_len, layers * sections, features), jnp.bfloat16),
            in_specs=[pl.BlockSpec(memory_space=pl.ANY), pl.BlockSpec(memory_space=pl.ANY)],
            out_specs=pl.BlockSpec(memory_space=pltpu.VMEM),
            scratch_shapes=[
                pltpu.SMEM((blocks,), jnp.int32),
                pltpu.SMEM((blocks,), jnp.int32),
                pltpu.VMEM((layers, tokens, features), jnp.float32),
                pltpu.VMEM((row_tiles, features // LANES, per_dev, *tile), jnp.float32),
                pltpu.VMEM((1, LANES), jnp.float32),
                pltpu.VMEM((groups, 1, LANES), jnp.float32),
                dma, dma, dma, dma, pltpu.SemaphoreType.REGULAR,
                *[dma((len(boxes),)) for _ in range(2)],
                *[dma((len(units),)) for _ in range(2)],
                *[pltpu.VMEM(inboxes[b], jnp.float32 if boxes[b][4] else jnp.bfloat16) for b in range(len(boxes))],
                *[pltpu.VMEM(shape, jnp.bfloat16) for shape in outboxes * 2],
                *[pltpu.VMEM(inboxes[b], jnp.bfloat16) for b in range(len(boxes)) if not boxes[b][4]],
            ],
            compiler_params=pltpu.CompilerParams(collective_id=0, has_side_effects=True),
            name="harvest",
        )(residuals, owners)
        return pl.pallas_call(
            store_kernel,
            out_shape=jax.ShapeDtypeStruct(received.shape, received.dtype),
            in_specs=[pl.BlockSpec(memory_space=pltpu.VMEM)],
            out_specs=pl.BlockSpec(memory_space=pl.ANY),
            scratch_shapes=[pltpu.SemaphoreType.DMA],
            name="store",
        )(pltpu.with_memory_space_constraint(received, pltpu.VMEM))

    in_specs = (P("section", "dp", None), P())
    out_specs = P(("section", "dp"), None, None)
    return jax.shard_map(on_device, mesh=mesh, in_specs=in_specs, out_specs=out_specs, check_vma=False)
```

time: 22.3 us -> 21.3 us (0.955)
  the two profiles are of different devices: /device:TPU:1 before, /device:TPU:0 now
where the time goes in v3:
time: 21.3 us; the launch traced here: 21.2 us
  Pallas kernels  21.2 us (100%)
    pallas_call x1, Pallas kernels, on_device(): pl.pallas_call(functools.partial(harvest_kernel, sections, groups, each),...  20.5 us
    pallas_call x1, Pallas kernels, on_device(): pl.pallas_call(store_kernel, out_shape=jax.ShapeDtypeStruct(received.shap...  0.71 us

profile of v3, /device:TPU:0, one launch (start us, length us, event | category | flops | bytes accessed | tf_op | source)
XLA Modules:
  0.0 21.2 jit_solution(14446840023495065949)
XLA Ops:
  0.0 20.5 %harvest.1.assembled = bf16[4,8,4096]{2,1,0:T(8,128)(2,1)S(1)} custom-call(f32[4,8,4096]{2,1,0:T(8,128)} %x_hbm.1, s32[32]{0:T(128)} %owners_hbm.1), custom_call_target="tpu_custom_call" | custom-call | tf_op jit(solution)/shard_map/harvest/pallas_call | solution.py:386
  20.5 0.7 %store.1 = bf16[4,8,4096]{2,1,0:T(8,128)(2,1)} custom-call(bf16[4,8,4096]{2,1,0:T(8,128)(2,1)S(1)} %harvest.1.assembled), custom_call_target="tpu_custom_call" | custom-call | tf_op jit(solution)/shard_map/store/pallas_call | solution.py:408

commit v4 on v3

--- a/solution.py
+++ b/solution.py
@@ -11,36 +11,32 @@
 LANES = 128
 SUBLANES = 8
 LAG = 8
-SHARE = 0
-JOINED = 1
-LI = 1
+SHARE = 2
 ABS = 2
-STAGED = 0
-LOW = (0, 1, 2)
 ORDL = 'near'
 ORDE = 'near'
-PRE = ((1,), (0,), (2,))
-STEPS = ((0, (0, 2)), (1, (0, 2, 3)), (0, ((1, 'a'), 3)), (2, (0, 2, 3)), (1, ((1, 'a'),)), (2, ((1, 'a'),)),
-         (0, ((1, 'b'),)), (1, ((1, 'b'),)), (2, ((1, 'b'),)))
+PRE = ((1, 'a'), (0, 'b'), (1, 'b'), (2, 'a'), (2, 'b'))
+ORDN = 'near'
+STEPS = ((0, (0, 2)), (1, (0, 2, 3)), (0, ((1, 'a'), 3)), (1, ((1, 'a'),)), (2, (0, 2, 3)), (2, ((1, 'a'),)), (0, ((1, 'b'),)), (1, ((1, 'b'),)), (2, ((1, 'b'),)))
 
 
 def layout(row_tiles, per_dev, each):
     share = per_dev // SHARE if SHARE else 0
-    boxes = [(True, None, 0, per_dev, True), (False, 0, 0, per_dev, True)]
-    units = [[0], [1]]
-    rest = []
+    boxes = [(True, None, 0, per_dev, True, None), (False, 0, 0, per_dev, True, None)]
     for piece in range(1, each):
         cut = share if piece == 1 else 0
         if cut:
-            boxes.append((False, piece, 0, cut, True))
-        boxes.append((False, piece, cut, per_dev, False))
-        rest.append(piece)
-    units += [rest] if JOINED and rest else [[p] for p in rest]
+            boxes.append((False, piece, 0, cut, True, 1))
+            boxes.append((False, piece, cut, per_dev, False, 1))
+            boxes.append((False, piece, 0, per_dev, False, 0))
+        else:
+            boxes.append((False, piece, 0, per_dev, False, None))
+    units = [[0], [1]] + ([list(range(1, each))] if each > 1 else [])
     return boxes, units
 
 
 def harvest_kernel(sections, groups, each, x_hbm, owners_hbm, out_ref, owners, inverse, xv, centered, part,
-                   parts, x_sem, o_sem, e_send, e_recv, ready, send1, recv1, send2, recv2, *buffers):
+                   parts, x_sem, o_sem, e_send, e_recv, send1, recv1, send2, recv2, *buffers):
     layers, tokens, features = x_hbm.shape
     pieces = features // LANES
     blocks = owners.shape[0]
@@ -82,9 +78,7 @@
 
     for t in range(4):
         for k in range(quarter):
-            if t == 0 and STAGED:
-                pl.when((plane == 1) | (plane == 0) if k else plane == 1)(lambda: signal(barrier, member(t, k)))
-            elif k:
+            if k:
                 signal(barrier, member(t, k))
             else:
                 pl.when(plane != t)(lambda: signal(barrier, member(t, k)))
@@ -133,7 +127,7 @@
             device_id=(section, group), device_id_type=MESH)
 
     def source(b, d):
-        half, piece, low, high, raw = boxes[b]
+        half, piece, low, high, raw, _ = boxes[b]
         if half:
             return centered.at[:, wide_chunks + lax.rem(d, side)]
         if not raw:
@@ -142,17 +136,25 @@
         return centered.at[pl.ds(lax.rem(at, row_tiles), 1), at // row_tiles, pl.ds(low, high - low)]
 
     def slot(b):
-        half, _, low, high, _ = boxes[b]
-        return pl.ds((spot if half else group) * (high - low), high - low)
-
-    def spread(*group_of, peers=None):
-        first = group_of[0]
-        if peers is None:
-            peers = [beside(k) for k in range(1, side)] if boxes[first][0] else circle(ORDE if boxes[first][4] else ORDL)
-        for d, b in [(d, b) for d in peers for b in group_of]:
-            pltpu.make_async_remote_copy(
-                src_ref=source(b, d), dst_ref=r1[b].at[:, slot(b)], send_sem=send1.at[b], recv_sem=recv1.at[b],
-                device_id=(section, d), device_id_type=MESH).start()
+        half, _, low, high, _, who = boxes[b]
+        return pl.ds((spot if half or who is not None else group) * (high - low), high - low)
+
+    def from_us(b, body):
+        who = boxes[b][5]
+        if who is None:
+            body()
+        else:
+            pl.when(upper == who)(body)
+
+    def post(b, d):
+        pltpu.make_async_remote_copy(
+            src_ref=source(b, d), dst_ref=r1[b].at[:, slot(b)], send_sem=send1.at[b], recv_sem=recv1.at[b],
+            device_id=(section, d), device_id_type=MESH).start()
+
+    def keep(b):
+        def body():
+            r1[b][:, slot(b)] = source(b, group)[...]
+        from_us(b, body)
 
     def circle(kind):
         if kind == 'near':
@@ -164,40 +166,20 @@
     early = [b for b in range(nb) if boxes[b][4]]
 
     def full_start():
-        for d in circle('near'):
+        for d in circle(ORDN):
             send_part(part, d, e_recv)
-        for bs in PRE:
-            bs = [b for b in bs if b in early]
-            if bs:
-                spread(*bs)
-
-    if STAGED:
-        some = (plane + 3) // 4
-        pl.semaphore_wait(barrier, side - 1 + sections - 1 + side * some)
-
-        @pl.when(plane == 0)
-        def _():
-            nearby = [beside(k) for k in range(1, side)]
-            distant = [across(k) for k in range(side)]
-            for d in nearby:
-                send_part(part, d, e_recv)
-            for b in LOW:
-                if b in early:
-                    spread(b, peers=nearby)
-            pl.semaphore_wait(ready, 1)
-            for d in distant:
-                send_part(part, d, e_recv)
-            for b in LOW:
-                if b in early and b:
-                    spread(b, peers=distant)
-
-        @pl.when(plane >= 1)
-        def _():
-            pl.when(plane == 1)(lambda: signal(ready, group - quarter))
-            full_start()
-    else:
-        pl.semaphore_wait(barrier, groups + sections - 2)
-        full_start()
+        for b, where in PRE:
+            if b not in early:
+                continue
+            peers = {'a': [across(k) for k in range(side)], 'b': [beside(k) for k in range(1, side)]}.get(where)
+
+            def body():
+                for d in peers or circle(ORDE):
+                    post(b, d)
+            from_us(b, body)
+
+    pl.semaphore_wait(barrier, groups + sections - 2)
+    full_start()
 
     load_owners.wait()
 
@@ -209,7 +191,7 @@
         inverse[o] = found
 
     for b in early:
-        r1[b][:, slot(b)] = source(b, group)[...]
+        keep(b)
     energies(groups - 1, e_recv).wait_recv()
     total = parts[0]
     for g in range(1, groups):
@@ -217,25 +199,51 @@
     energy = jnp.sum(jnp.where(own_lanes, total, 0.0), axis=1, keepdims=True)
     scale = 1.0 / jnp.sqrt(energy * (1.0 / (tokens * groups * features)) + 1.0)
 
-    for b, out in late.items():
-        _, piece, low, high, _ = boxes[b]
+    def fill(b):
+        _, piece, low, high, _, _ = boxes[b]
         for d in range(groups):
             chunk, tile = divmod(d * each + piece, row_tiles)
             for j in range(low, high):
-                out[0, d * (high - low) + j - low] = (centered[tile, chunk, j] * scale).astype(jnp.bfloat16)
-        if not LI:
-            spread(b)
-    if late and LI:
-        spread(*late)
-    for b, out in late.items():
-        r1[b][:, slot(b)] = out[:, slot(b)]
-
-    def arrived(b):
-        half, _, low, high, _ = boxes[b]
-        span = r1[b].at[:, pl.ds(0, ((side if half else groups) - 1) * (high - low))]
+                late[b][0, d * (high - low) + j - low] = (centered[tile, chunk, j] * scale).astype(jnp.bfloat16)
+
+    def finish(who):
+        ours = [b for b in late if boxes[b][5] in (None, who)]
+        for b in ours:
+            fill(b)
+        for d in circle(ORDL):
+            for b in ours:
+                post(b, d)
+
+    if any(boxes[b][5] is not None for b in late):
+        for who in range(2):
+            pl.when(upper == who)(functools.partial(finish, who))
+    elif late:
+        finish(None)
+    for b in late:
+        keep(b)
+
+    def span_of(b, count):
+        wanted, raw = count * (boxes[b][3] - boxes[b][2]), boxes[b][4]
+        model = b if wanted <= r1[b].shape[1] else next(
+            m for m in range(nb) if boxes[m][4] == raw and r1[m].shape[0] == 1 and r1[m].shape[1] >= wanted)
+        return r1[model].at[:, pl.ds(0, wanted)]
+
+    def arrival(b, count):
+        span = span_of(b, count)
         return pltpu.make_async_remote_copy(
             src_ref=span, dst_ref=span, send_sem=send1.at[b], recv_sem=recv1.at[b],
             device_id=(section, group), device_id_type=MESH)
+
+    def await_box(b):
+        half, _, _, _, _, who = boxes[b]
+        if who is None:
+            arrival(b, (side if half else groups) - 1).wait_recv()
+        else:
+            pl.when(upper == who)(lambda: arrival(b, side - 1).wait_recv())
+            pl.when(upper != who)(lambda: arrival(b, side).wait_recv())
+
+    def await_sent(b):
+        from_us(b, lambda: arrival(b, (side if boxes[b][0] else groups) - 1).wait_send())
 
     def delivered(u):
         span = r2[u].at[pl.ds(0, sections * groups - 1)]
@@ -267,9 +275,11 @@
             else:
                 cut = boxes[which[0]][3]
                 d, j = at // per_dev, lax.rem(at, per_dev)
-                first = scaled(r1[which[0]][0, d * cut + lax.rem(j, cut)])
-                second = r1[which[1]][0, d * (per_dev - cut) + lax.rem(j, per_dev - cut)]
-                got.append(jnp.where(j < cut, first, second))
+                place = lax.rem(d, side)
+                first = scaled(r1[which[0]][0, place * cut + lax.rem(j, cut)])
+                second = r1[which[1]][0, place * (per_dev - cut) + lax.rem(j, per_dev - cut)]
+                third = r1[which[2]][0, place * per_dev + j]
+                got.append(jnp.where(d < side, third, jnp.where(j < cut, first, second)))
         return got
 
     def deliver(u, planes):
@@ -325,7 +335,7 @@
     for u, planes in steps:
         if u not in seen:
             for b in needs(u):
-                arrived(b).wait_recv()
+                await_box(b)
             seen.append(u)
         deliver(u, planes)
     for u in seen:
@@ -355,7 +365,7 @@
 
     energies(groups - 1, e_recv).wait_send()
     for b in range(nb):
-        arrived(b).wait_send()
+        await_sent(b)
     for u in range(nu):
         delivered(u).wait_send()
 
@@ -380,8 +390,8 @@
         boxes, units = layout(row_tiles, per_dev, each)
         tile = (SUBLANES, LANES)
         dma = pltpu.SemaphoreType.DMA
-        inboxes = [(row_tiles if half else 1, (side if half else groups) * (high - low), *tile)
-                   for half, _, low, high, _ in boxes]
+        inboxes = [(row_tiles if half else 1, (side if half or who is not None else groups) * (high - low), *tile)
+                   for half, _, low, high, _, who in boxes]
         outboxes = [(blocks, row_tiles if u == 0 else 1 if u == 1 else len(units[u]), *tile) for u in range(len(units))]
         received = pl.pallas_call(
             functools.partial(harvest_kernel, sections, groups, each),
@@ -395,12 +405,12 @@
                 pltpu.VMEM((row_tiles, features // LANES, per_dev, *tile), jnp.float32),
                 pltpu.VMEM((1, LANES), jnp.float32),
                 pltpu.VMEM((groups, 1, LANES), jnp.float32),
-                dma, dma, dma, dma, pltpu.SemaphoreType.REGULAR,
+                dma, dma, dma, dma,
                 *[dma((len(boxes),)) for _ in range(2)],
                 *[dma((len(units),)) for _ in range(2)],
                 *[pltpu.VMEM(inboxes[b], jnp.float32 if boxes[b][4] else jnp.bfloat16) for b in range(len(boxes))],
                 *[pltpu.VMEM(shape, jnp.bfloat16) for shape in outboxes * 2],
-                *[pltpu.VMEM(inboxes[b], jnp.bfloat16) for b in range(len(boxes)) if not boxes[b][4]],
+                *[pltpu.VMEM((1, groups * (b[3] - b[2]), *tile), jnp.bfloat16) for b in boxes if not b[4]],
             ],
             compiler_params=pltpu.CompilerParams(collective_id=0, has_side_effects=True),
             name="harvest",

time: 21.3 us -> 21.1 us (level)
  Pallas kernels: 21.2 us -> 20.9 us
    pallas_call x1, Pallas kernels: 20.5 us -> 20.2 us  [on_device(): pl.pallas_call(functools.partial(harvest_kernel, sections, groups, each),...]
where the time goes in v4:
time: 21.1 us; the launch traced here: 20.9 us
  Pallas kernels  20.9 us (99%)
    pallas_call x1, Pallas kernels, on_device(): pl.pallas_call(functools.partial(harvest_kernel, sections, groups, each),...  20.2 us
    pallas_call x1, Pallas kernels, on_device(): pl.pallas_call(store_kernel, out_shape=jax.ShapeDtypeStruct(received.shap...  0.71 us

profile of v4, /device:TPU:0, one launch (start us, length us, event | category | flops | bytes accessed | tf_op | source)
XLA Modules:
  0.0 20.9 jit_solution(6089230327250955279)
XLA Ops:
  0.0 20.2 %harvest.1.assembled = bf16[4,8,4096]{2,1,0:T(8,128)(2,1)S(1)} custom-call(f32[4,8,4096]{2,1,0:T(8,128)} %x_hbm.1, s32[32]{0:T(128)} %owners_hbm.1), custom_call_target="tpu_custom_call" | custom-call | tf_op jit(solution)/shard_map/harvest/pallas_call | solution.py:396
  20.2 0.7 %store.1 = bf16[4,8,4096]{2,1,0:T(8,128)(2,1)} custom-call(bf16[4,8,4096]{2,1,0:T(8,128)(2,1)S(1)} %harvest.1.assembled), custom_call_target="tpu_custom_call" | custom-call | tf_op jit(solution)/shard_map/store/pallas_call | solution.py:418

commit v5 on v4

--- a/solution.py
+++ b/solution.py
@@ -12,23 +12,20 @@
 SUBLANES = 8
 LAG = 8
 SHARE = 2
-ABS = 2
-ORDL = 'near'
-ORDE = 'near'
+WHO = 1
 PRE = ((1, 'a'), (0, 'b'), (1, 'b'), (2, 'a'), (2, 'b'))
-ORDN = 'near'
 STEPS = ((0, (0, 2)), (1, (0, 2, 3)), (0, ((1, 'a'), 3)), (1, ((1, 'a'),)), (2, (0, 2, 3)), (2, ((1, 'a'),)), (0, ((1, 'b'),)), (1, ((1, 'b'),)), (2, ((1, 'b'),)))
 
 
 def layout(row_tiles, per_dev, each):
-    share = per_dev // SHARE if SHARE else 0
+    share = per_dev // SHARE
     boxes = [(True, None, 0, per_dev, True, None), (False, 0, 0, per_dev, True, None)]
     for piece in range(1, each):
         cut = share if piece == 1 else 0
         if cut:
-            boxes.append((False, piece, 0, cut, True, 1))
-            boxes.append((False, piece, cut, per_dev, False, 1))
-            boxes.append((False, piece, 0, per_dev, False, 0))
+            boxes.append((False, piece, 0, cut, True, WHO))
+            boxes.append((False, piece, cut, per_dev, False, WHO))
+            boxes.append((False, piece, 0, per_dev, False, 1 - WHO))
         else:
             boxes.append((False, piece, 0, per_dev, False, None))
     units = [[0], [1]] + ([list(range(1, each))] if each > 1 else [])
@@ -156,30 +153,19 @@
             r1[b][:, slot(b)] = source(b, group)[...]
         from_us(b, body)
 
-    def circle(kind):
-        if kind == 'near':
-            return [peer_of(p) for p in sorted(range(1, groups), key=lambda p: min(p, groups - p))]
-        if kind == 'rot':
-            return [peer_of(p) for p in range(1, groups)]
-        return [across(k) for k in range(side)] + [beside(k) for k in range(1, side)]
+    around = [peer_of(p) for p in sorted(range(1, groups), key=lambda p: min(p, groups - p))]
 
     early = [b for b in range(nb) if boxes[b][4]]
 
-    def full_start():
-        for d in circle(ORDN):
-            send_part(part, d, e_recv)
-        for b, where in PRE:
-            if b not in early:
-                continue
-            peers = {'a': [across(k) for k in range(side)], 'b': [beside(k) for k in range(1, side)]}.get(where)
-
-            def body():
-                for d in peers or circle(ORDE):
+    pl.semaphore_wait(barrier, groups + sections - 2)
+    for d in around:
+        send_part(part, d, e_recv)
+    for b, where in PRE:
+        if b in early:
+            def issue():
+                for d in [across(k) for k in range(side)] if where == 'a' else [beside(k) for k in range(1, side)]:
                     post(b, d)
-            from_us(b, body)
-
-    pl.semaphore_wait(barrier, groups + sections - 2)
-    full_start()
+            from_us(b, issue)
 
     load_owners.wait()
 
@@ -210,7 +196,7 @@
         ours = [b for b in late if boxes[b][5] in (None, who)]
         for b in ours:
             fill(b)
-        for d in circle(ORDL):
+        for d in around:
             for b in ours:
                 post(b, d)
 
@@ -279,29 +265,23 @@
                 first = scaled(r1[which[0]][0, place * cut + lax.rem(j, cut)])
                 second = r1[which[1]][0, place * (per_dev - cut) + lax.rem(j, per_dev - cut)]
                 third = r1[which[2]][0, place * per_dev + j]
-                got.append(jnp.where(d < side, third, jnp.where(j < cut, first, second)))
+                got.append(jnp.where(d // side == WHO, jnp.where(j < cut, first, second), third))
         return got
 
     def deliver(u, planes):
-        if ABS == 1:
-            keys = [(h, c, q) for q in range(sections) for h in range(quarter // 2) for c in range(2)]
-        elif ABS == 2:
-            keys = [(h, c, q) for h in range(quarter // 2) for q in range(sections) for c in range(2)]
-        elif ABS == 3:
-            keys = [(h, c, q) for h in range(quarter // 2) for c in range(2) for q in range(sections)]
-        else:
-            keys = [(h, c, q) for h in range(quarter // 2) for c in range(2) for q in range(sections)]
+        keys = [(h, c, q) for q in range(sections) for h in range(quarter // 2) for c in range(2)]
         routes = []
         for t in planes:
             t, part = t if isinstance(t, tuple) else (t, None)
             routes += [(t, k, k[2]) for k in keys if part is None or (part == 'a') == (k[0] == 0 and k[2] == 0)]
+        by_plane = {}
+        for r in routes:
+            by_plane.setdefault(r[0], []).append(r)
+        routes = [r for n in range(len(keys)) for rs in by_plane.values() for r in rs[n:n + 1]]
 
         def place(t, k, q):
             h, c, _ = k
-            if ABS:
-                sec, d = jnp.int32(q), t * quarter + h * 2 + lax.rem(corner + c, 2)
-            else:
-                sec, d = lax.rem(section + q, sections), t * quarter + lax.rem(corner + h * 2 + c, quarter)
+            sec, d = jnp.int32(q), t * quarter + h * 2 + lax.rem(corner + c, 2)
             return sec, d, sec * groups + d
 
         def select(t, k, q):
@@ -317,12 +297,10 @@
                     src_ref=s2[u].at[o], dst_ref=r2[u].at[me], send_sem=send2.at[u], recv_sem=recv2.at[u],
                     device_id=(sec, d), device_id_type=MESH).start()
             h, c, _ = k
-            if ABS and not c:
+            if c:
+                go()
+            else:
                 pl.when((plane != t) | (section != q) | (corner // 2 != h))(go)
-            elif not ABS and not (h or c or q):
-                pl.when(plane != t)(go)
-            else:
-                go()
 
         for n in range(len(routes) + LAG):
             if n < len(routes):

time: 21.1 us -> 21.1 us (level)
  the two profiles are of different devices: /device:TPU:0 before, /device:TPU:11 now
where the time goes in v5:
time: 21.1 us; the launch traced here: 20.9 us
  Pallas kernels  20.9 us (99%)
    pallas_call x1, Pallas kernels, on_device(): pl.pallas_call(functools.partial(harvest_kernel, sections, groups, each),...  20.2 us
    pallas_call x1, Pallas kernels, on_device(): pl.pallas_call(store_kernel, out_shape=jax.ShapeDtypeStruct(received.shap...  0.71 us

profile of v5, /device:TPU:11, one launch (start us, length us, event | category | flops | bytes accessed | tf_op | source)
XLA Modules:
  0.0 20.9 jit_solution(12277320145295199222)
XLA Ops:
  0.0 20.2 %harvest.1.assembled = bf16[4,8,4096]{2,1,0:T(8,128)(2,1)S(1)} custom-call(f32[4,8,4096]{2,1,0:T(8,128)} %x_hbm.1, s32[32]{0:T(128)} %owners_hbm.1), custom_call_target="tpu_custom_call" | custom-call | tf_op jit(solution)/shard_map/harvest/pallas_call | solution.py:374
  20.2 0.7 %store.1 = bf16[4,8,4096]{2,1,0:T(8,128)(2,1)} custom-call(bf16[4,8,4096]{2,1,0:T(8,128)(2,1)S(1)} %harvest.1.assembled), custom_call_target="tpu_custom_call" | custom-call | tf_op jit(solution)/shard_map/store/pallas_call | solution.py:396

commit v6 on v5

--- a/solution.py
+++ b/solution.py
@@ -196,7 +196,10 @@
         ours = [b for b in late if boxes[b][5] in (None, who)]
         for b in ours:
             fill(b)
-        for d in around:
+        order = around
+        if who == 0:
+            order = [across(k) for k in range(side)] + [beside(k) for k in range(1, side)]
+        for d in order:
             for b in ours:
                 post(b, d)
 

time: 21.1 us -> 21 us (level)
  the two profiles are of different devices: /device:TPU:11 before, /device:TPU:0 now
where the time goes in v6:
time: 21 us; the launch traced here: 20.8 us
  Pallas kernels  20.8 us (99%)
    pallas_call x1, Pallas kernels, on_device(): pl.pallas_call(functools.partial(harvest_kernel, sections, groups, each),...  20.1 us
    pallas_call x1, Pallas kernels, on_device(): pl.pallas_call(store_kernel, out_shape=jax.ShapeDtypeStruct(received.shap...  0.71 us

profile of v6, /device:TPU:0, one launch (start us, length us, event | category | flops | bytes accessed | tf_op | source)
XLA Modules:
  0.0 20.8 jit_solution(4217057637466263359)
XLA Ops:
  0.0 20.1 %harvest.1.assembled = bf16[4,8,4096]{2,1,0:T(8,128)(2,1)S(1)} custom-call(f32[4,8,4096]{2,1,0:T(8,128)} %x_hbm.1, s32[32]{0:T(128)} %owners_hbm.1), custom_call_target="tpu_custom_call" | custom-call | tf_op jit(solution)/shard_map/harvest/pallas_call | solution.py:377
  20.1 0.7 %store.1 = bf16[4,8,4096]{2,1,0:T(8,128)(2,1)} custom-call(bf16[4,8,4096]{2,1,0:T(8,128)(2,1)S(1)} %harvest.1.assembled), custom_call_target="tpu_custom_call" | custom-call | tf_op jit(solution)/shard_map/store/pallas_call | solution.py:399

commit v7 on v6

--- a/solution.py
+++ b/solution.py
@@ -198,7 +198,7 @@
             fill(b)
         order = around
         if who == 0:
-            order = [across(k) for k in range(side)] + [beside(k) for k in range(1, side)]
+            order = [member(t, k) for t in (3, 2) for k in range(quarter)] + [beside(k) for k in range(1, side)]
         for d in order:
             for b in ours:
                 post(b, d)

time: 21 us -> 21 us (level)
  no operation moved by 1% of the time
where the time goes in v7:
time: 21 us; the launch traced here: 20.9 us
  Pallas kernels  20.9 us (100%)
    pallas_call x1, Pallas kernels, on_device(): pl.pallas_call(functools.partial(harvest_kernel, sections, groups, each),...  20.1 us
    pallas_call x1, Pallas kernels, on_device(): pl.pallas_call(store_kernel, out_shape=jax.ShapeDtypeStruct(received.shap...  0.71 us

profile of v7, /device:TPU:0, one launch (start us, length us, event | category | flops | bytes accessed | tf_op | source)
XLA Modules:
  0.0 20.9 jit_solution(1421515238960878790)
XLA Ops:
  0.0 20.1 %harvest.1.assembled = bf16[4,8,4096]{2,1,0:T(8,128)(2,1)S(1)} custom-call(f32[4,8,4096]{2,1,0:T(8,128)} %x_hbm.1, s32[32]{0:T(128)} %owners_hbm.1), custom_call_target="tpu_custom_call" | custom-call | tf_op jit(solution)/shard_map/harvest/pallas_call | solution.py:377
  20.2 0.7 %store.1 = bf16[4,8,4096]{2,1,0:T(8,128)(2,1)} custom-call(bf16[4,8,4096]{2,1,0:T(8,128)(2,1)S(1)} %harvest.1.assembled), custom_call_target="tpu_custom_call" | custom-call | tf_op jit(solution)/shard_map/store/pallas_call | solution.py:399
